TPU v7x, 256 devices: a whole 4x4x8 slice. The times are simulated.
256 devices in a mesh: seq: 8 (over z), tensor: 8 (over x, y_hi), dp: 4 (over y_lo, core).
Axes of the slice: x: 4, y: 4 (y_hi: 2, y_lo: 2; y = y_hi * 2 + y_lo), z: 8, core: 2. Of those that a mesh axis runs over, the one named last changes fastest.
Arguments:
- tokens: bfloat16 [4, 2048, 3072], P('dp', 'seq'), may hold values from -6 to 6
- cotangent: bfloat16 [4, 2048, 3072], P('dp', 'seq'), may hold values from -6 to 6
- qkv_weight: bfloat16 [3072, 3, 3072], P(('seq', 'dp'), None, 'tensor'), may hold values from -0.109375 to 0.109375
- out_weight: bfloat16 [3072, 3072], P(('seq', 'dp'), 'tensor'), may hold values from -0.109375 to 0.109375
Outputs:
- qkv_grad: float32 [3072, 3, 3072], P(('seq', 'dp'), None, 'tensor')
- out_grad: float32 [3072, 3072], P(('seq', 'dp'), 'tensor')
- branch_grad: bfloat16 [4, 2048, 3072], P('dp', 'seq', 'tensor')
All inputs are finite; a program needn't handle non-finite values.
Results may differ from a plain program's by a relative error of at most 0.025.
Values may be sent and summed in bfloat16 or wider, within the bound.
No kernel may reach another device: no remote copies, remote signals or barrier semaphores. Data moves between devices by JAX's collectives and lax.ppermute only.
A program may use at most 128 MiB of HBM per device.

v0:
```python
import jax
import jax.numpy as jnp
from jax import lax
from jax.sharding import PartitionSpec as P

HD = 128
epsilon = 1e-06


def sent_together(arrays, axis, dim, along):
    both = jnp.concatenate(arrays, axis=along)
    result, at, done = (lax.all_gather(both, axis, axis=dim, tiled=True), 0, [])
    for a in arrays:
        done.append(lax.slice_in_dim(result, at, at + a.shape[along], axis=along))
        at += a.shape[along]
    return tuple(done)


def split_up(shard, dim, size):
    before, after = (shard.shape[:dim], shard.shape[dim + 1 :])
    return jnp.moveaxis(shard.reshape(*before, size, -1, *after), dim, 0)


def summed_on_arrival(shard, axis, dim):
    size = lax.axis_size(axis)
    pieces = lax.all_to_all(split_up(shard, dim, size), axis, 0, 0, tiled=True)
    return jnp.sum(pieces.astype(jnp.float32), axis=0)


def copy_for_each(shard, axis):
    copies = jnp.broadcast_to(shard, (lax.axis_size(axis), *shard.shape))
    return lax.all_to_all(copies, axis, split_axis=0, concat_axis=0, tiled=True)


def taken_together(shard, axis):
    everything = copy_for_each(shard, axis)
    return jnp.sum(everything, axis=0)


def in_one(arrays, axis):
    ends = [0]
    for a in arrays:
        ends.append(ends[-1] + a.size)
    subtotal = taken_together(jnp.concatenate([a.ravel() for a in arrays]), axis)
    return tuple((subtotal[b:e].reshape(a.shape) for a, b, e in zip(arrays, ends, ends[1:])))


def normalize(values):
    average = jnp.mean(values, axis=-1, keepdims=True)
    centered = values - average
    inverse = lax.rsqrt(jnp.mean(centered * centered, axis=-1, keepdims=True) + epsilon)
    return (centered * inverse, inverse)


def normalize_back(gradient, normed, inverse):
    mean_grad = jnp.mean(gradient, axis=-1, keepdims=True)
    mean_both = jnp.mean(gradient * normed, axis=-1, keepdims=True)
    return (gradient - mean_grad - normed * mean_both) * inverse


def local(tokens, cotangent, qkv_weight, out_weight):
    row_count = tokens.shape[1]
    feature_count = tokens.shape[2]
    column_count = out_weight.shape[1]
    head_count = column_count // HD
    score_scale = HD ** (-0.5)
    own_rows = qkv_weight.shape[0]
    grad_rows = cotangent[0]
    normed, inverse = normalize(tokens[0].astype(jnp.float32))
    unit_low = normed.astype(jnp.bfloat16)
    flat_weight = qkv_weight.reshape(own_rows, 3 * column_count)
    piece_qkv, piece_out = sent_together((flat_weight, out_weight), ("seq", "dp"), 0, 1)
    piece_rows = piece_qkv.shape[0]
    left_rows = unit_low
    right_rows = grad_rows
    projected = jnp.dot(left_rows, piece_qkv, preferred_element_type=jnp.float32)
    attended_grad = jnp.dot(right_rows, piece_out, preferred_element_type=jnp.float32)
    full_qkv = piece_qkv
    projected, attended_grad, full_qkv = (projected, attended_grad, full_qkv)
    query_unit, query_inv = normalize(
        projected[:, :column_count].reshape(row_count, head_count, HD)
    )
    key_unit, key_inv = normalize(
        projected[:, column_count : 2 * column_count].reshape(row_count, head_count, HD)
    )
    query_low = query_unit.astype(jnp.bfloat16)
    key_value = jnp.stack(
        [
            key_unit.astype(jnp.bfloat16).reshape(row_count, column_count),
            projected[:, 2 * column_count :].astype(jnp.bfloat16),
        ]
    )
    grad_low = attended_grad.astype(jnp.bfloat16).reshape(row_count, head_count, HD)

    def scores_of(key_rows):
        piece_rows = key_rows.shape[0]
        return (
            jnp.einsum(
                "qhd,khd->hqk",
                query_low,
                key_rows.reshape(piece_rows, head_count, HD),
                preferred_element_type=jnp.float32,
            )
            * score_scale
        )

    every_pair = lax.all_gather(key_value, "seq", axis=1, tiled=True)
    piece_rows = every_pair.shape[1]
    exponent = jnp.exp(scores_of(every_pair[0]))
    add_exp_total = jnp.sum(exponent, axis=-1)
    weighted = jnp.einsum(
        "hqk,khd->qhd",
        exponent.astype(jnp.bfloat16),
        every_pair[1].reshape(piece_rows, head_count, HD),
        preferred_element_type=jnp.float32,
    )
    exp_total, weighted = (add_exp_total, weighted)
    attended_low = (weighted / exp_total.T[:, :, None]).astype(jnp.bfloat16)
    row_delta = jnp.sum(grad_low.astype(jnp.float32) * attended_low.astype(jnp.float32), axis=-1)
    piece_rows = every_pair.shape[1]
    key_rows = every_pair[0].reshape(piece_rows, head_count, HD)
    value_rows = every_pair[1].reshape(piece_rows, head_count, HD)
    probability = jnp.exp(scores_of(every_pair[0])) / exp_total[:, :, None]
    prob_grad = jnp.einsum("qhd,khd->hqk", grad_low, value_rows, preferred_element_type=jnp.float32)
    grad_score = (probability * (prob_grad - row_delta.T[:, :, None]) * score_scale).astype(
        jnp.bfloat16
    )
    query_part = jnp.einsum(
        "hqk,khd->qhd", grad_score, key_rows, preferred_element_type=jnp.float32
    )
    key_part = jnp.einsum("hqk,qhd->khd", grad_score, query_low, preferred_element_type=jnp.float32)
    value_part = jnp.einsum(
        "hqk,qhd->khd",
        probability.astype(jnp.bfloat16),
        grad_low,
        preferred_element_type=jnp.float32,
    )
    every_grad = jnp.stack(
        [key_part.reshape(piece_rows, column_count), value_part.reshape(piece_rows, column_count)]
    )
    pair_grad = lax.psum_scatter(
        every_grad.astype(jnp.bfloat16), "seq", scatter_dimension=1, tiled=True
    ).astype(jnp.float32)
    query_back = normalize_back(query_part, query_unit, query_inv)
    key_back = normalize_back(pair_grad[0].reshape(row_count, head_count, HD), key_unit, key_inv)
    qkv_low = jnp.concatenate(
        [
            query_back.reshape(row_count, column_count),
            key_back.reshape(row_count, column_count),
            pair_grad[1],
        ],
        axis=1,
    ).astype(jnp.bfloat16)
    inner_grad = jnp.einsum("rc,dc->rd", qkv_low, full_qkv, preferred_element_type=jnp.float32)
    attended_flat = attended_low.reshape(row_count, column_count)
    share_width = feature_count // lax.axis_size("tensor")
    own_share = summed_on_arrival(inner_grad.astype(jnp.bfloat16), "tensor", 1)
    offset = lax.axis_index("tensor") * share_width
    unit_own = lax.dynamic_slice_in_dim(normed, offset, share_width, 1)
    row_sums = in_one(
        (
            jnp.sum(own_share, axis=1, keepdims=True),
            jnp.sum(own_share * unit_own, axis=1, keepdims=True),
        ),
        "tensor",
    )
    branch = (
        own_share - row_sums[0] / feature_count - unit_own * (row_sums[1] / feature_count)
    ) * inverse
    left_rows = unit_low
    right_rows = grad_rows
    qkv_term = jnp.einsum(
        "rd,rc->dc", left_rows, qkv_low, preferred_element_type=jnp.float32
    ).reshape(lax.axis_size(("seq", "dp")) * own_rows, 3, column_count)
    out_term = jnp.einsum(
        "rd,rc->dc", right_rows, attended_flat, preferred_element_type=jnp.float32
    )
    summed = lax.psum_scatter(
        jnp.concatenate([qkv_term, out_term[:, None, :]], axis=1).astype(jnp.bfloat16),
        ("seq", "dp"),
        scatter_dimension=0,
        tiled=True,
    ).astype(jnp.float32)
    return (summed[:, :3], summed[:, 3], branch.astype(jnp.bfloat16)[None])


def solution(mesh):
    return jax.shard_map(
        local,
        mesh=mesh,
        in_specs=(
            P("dp", "seq", None),
            P("dp", "seq", None),
            P(("seq", "dp"), None, "tensor"),
            P(("seq", "dp"), "tensor"),
        ),
        out_specs=(
            P(("seq", "dp"), None, "tensor"),
            P(("seq", "dp"), "tensor"),
            P("dp", "seq", "tensor"),
        ),
        check_vma=False,
    )
```

profile of v0, /device:TPU:16, one launch (start us, length us, event | category | flops | bytes accessed | tf_op | source)
XLA Modules:
  0.0 414.2 jit_solution(13253095489150140398)
XLA Ops:
  12.4 73.2 %all-gather.3.cloned.1.call-done = bf16[3072,1536]{1,0:T(8,128)(2,1)} async-done(((bf16[96,1536]{1,0:T(8,128)(2,1)}), bf16[3072,1536]{1,0:T(8,128)(2,1)}) %all-gather.3.cloned.1.call-update) | async-done | bytes 9437200 | tf_op jit(solution)/shard_map/all_gather | solution.py:12
  85.5 5.3 %fusion.2 = f32[256,1152]{1,0:T(8,128)S(1)} fusion(bf16[3072,1536]{1,0:T(8,128)(2,1)} %all-gather.3.cloned.1.call-done, bf16[1,256,3072]{2,1,0:T(8,128)(2,1)S(1)} %copy-done.1, f32[256]{0:T(256)S(1)} %add_rsqrt_fusion.2, f32[256]{0:T(256)S(1)} %broadcast_multiply_fusion.6), kind=kOutput, calls=%fused_computation.5 | convolution fusion | flops 1815085056 | bytes 9832448 | tf_op jit(solution)/shard_map/dot_general | solution.py:76
  104.7 3.2 fusion.38
  107.8 40.1 %all-gather.5.cloned.1.call-done = bf16[2,2048,384]{2,1,0:T(8,128)(2,1)} async-done(((bf16[2,256,384]{2,1,0:T(8,128)(2,1)}), bf16[2,2048,384]{2,1,0:T(8,128)(2,1)}) %all-gather.5.cloned.1.call-update) | async-done | bytes 3145744 | tf_op jit(solution)/shard_map/all_gather | solution.py:107
  147.9 3.9 fusion.64
  151.8 2.6 copy.93
  154.4 2.6 copy.97
  157.0 2.8 fusion.6
  159.8 2.6 fusion.22
  164.3 2.5 multiply_convert_fusion
  170.2 2.6 copy.100
  172.8 2.6 copy.101
  175.4 3.9 pad_maximum_fusion.1
  179.5 3.6 fusion.63
  185.7 3.4 fusion.7
  189.0 36.0 %reduce-scatter.3.cloned.1.call-done = bf16[2,256,384]{2,1,0:T(8,128)(2,1)} async-done(((bf16[2,2048,384]{2,1,0:T(8,128)(2,1)}), bf16[2,256,384]{2,1,0:T(8,128)(2,1)}) %reduce-scatter.3.cloned.1.call-update) | async-done | bytes 393232 | tf_op jit(solution)/shard_map/reduce_scatter | solution.py:141
  240.8 5.7 %convolution_convert_fusion = bf16[3072,3,384]{2,0,1:T(8,128)(2,1)} fusion(bf16[3,384,256]{2,1,0:T(8,128)(2,1)} %bitcast.114, bf16[1,256,3072]{2,1,0:T(8,128)(2,1)S(1)} %copy-done.1, f32[256]{0:T(256)S(1)} %copy-done.14, f32[256]{0:T(256)S(1)} %copy-done.12), kind=kOutput, calls=%fused_computation.7 | convolution fusion | flops 1818624000 | bytes 9242624 | tf_op jit(solution)/shard_map/rd,rc->dc/dot_general | solution.py:172
  246.5 8.4 %pad_maximum_fusion = bf16[3072,4,384]{2,0,1:T(8,128)(2,1)} fusion(bf16[3072,1,384]{2,0,1:T(8,128)(2,1)} %fusion.7, bf16[3072,3,384]{2,0,1:T(8,128)(2,1)} %convolution_convert_fusion), kind=kLoop, calls=%fused_computation | loop fusion | flops 4718592 | bytes 18874368 | tf_op jit(solution)/shard_map/concatenate | solution.py:179
  255.9 5.3 %fusion.8 = bf16[256,3072]{1,0:T(8,128)(2,1)S(1)} fusion(bf16[3072,1536]{1,0:T(8,128)(2,1)} %all-gather.3.cloned.1.call-done, bf16[256,384]{1,0:T(8,128)(2,1)} %get-tuple-element.14, bf16[256,384]{1,0:T(8,128)(2,1)S(1)} %copy-done.8, bf16[256,384]{1,0:T(8,128)(2,1)S(1)} %copy-done.9), kind=kOutput, calls=%fused_computation.18 | convolution fusion | flops 1814495232 | bytes 9240576 | tf_op jit(solution)/shard_map/rc,dc->rd/dot_general | solution.py:154
  262.6 7.3 %all-to-all-start = ((bf16[8,256,384]{2,1,0:T(8,128)(2,1)}), bf16[8,256,384]{2,1,0:T(8,128)(2,1)}, u32[]{:S(2)}, u32[]{:S(2)}) async-start(bf16[8,256,384]{2,1,0:T(8,128)(2,1)} %bitcast.107), calls=%async_computation.2 | async-start | bytes 3145728 | tf_op jit(solution)/shard_map/all_to_all | solution.py:26
  269.9 2.3 fusion.14
  272.2 17.6 %all-to-all-done = bf16[8,256,384]{2,1,0:T(8,128)(2,1)} async-done(((bf16[8,256,384]{2,1,0:T(8,128)(2,1)}), bf16[8,256,384]{2,1,0:T(8,128)(2,1)}, u32[]{:S(2)}, u32[]{:S(2)}) %all-to-all-start) | async-done | bytes 1572896 | tf_op jit(solution)/shard_map/all_to_all | solution.py:26
  292.8 12.0 %all_to_all.11 = f32[8,1,512]{2,1,0:T(1,128)S(1)} all-to-all(f32[8,1,512]{2,1,0:T(1,128)S(1)} %broadcast_in_dim.8), channel_id=1, replica_groups=mesh['seq'=8,'tensor'=8,'dp'=4] {'tensor'}, dimensions={0} | all-to-all | bytes 32768 | tf_op jit(solution)/shard_map/all_to_all | solution.py:32
  306.7 97.6 %reduce-scatter.5.cloned.1.call-done = bf16[96,4,384]{2,0,1:T(8,128)(2,1)} async-done(((bf16[3072,4,384]{2,0,1:T(8,128)(2,1)}), bf16[96,4,384]{2,0,1:T(8,128)(2,1)}) %reduce-scatter.5.cloned.1.call-update) | async-done | bytes 294928 | tf_op jit(solution)/shard_map/reduce_scatter | solution.py:178
  (89 shorter events, 53.2 us)
Async XLA Ops:
  7.2 97.5 %copy-start = (bf16[1,256,3072]{2,1,0:T(8,128)(2,1)S(1)}, bf16[1,256,3072]{2,1,0:T(8,128)(2,1)}, u32[]{:S(2)}) copy-start(bf16[1,256,3072]{2,1,0:T(8,128)(2,1)} %param.5) | copy-start | bytes 4718596
  7.2 4.6 %copy-start.1 = (bf16[1,256,3072]{2,1,0:T(8,128)(2,1)S(1)}, bf16[1,256,3072]{2,1,0:T(8,128)(2,1)}, u32[]{:S(2)}) copy-start(bf16[1,256,3072]{2,1,0:T(8,128)(2,1)} %param.4) | copy-start | bytes 4718596
  7.2 78.3 %all-gather.3.cloned.1.call-start = ((), (), s32[]{:S(2)}) async-start(), calls=%async_computation.4 | async-start | bytes 9732096 | tf_op jit(solution)/shard_map/all_gather | solution.py:12
  10.0 137.9 %all-gather.5.cloned.1.call-start = ((), (), s32[]{:S(2)}) async-start(), calls=%async_computation.5 | async-start | bytes 3538944 | tf_op jit(solution)/shard_map/all_gather | solution.py:107
  11.8 79.0 %copy-start.11 = (f32[256]{0:T(256)}, f32[256]{0:T(256)S(1)}, u32[]{:S(2)}) copy-start(f32[256]{0:T(256)S(1)} %broadcast_multiply_fusion.6) | copy-start | bytes 3076
  12.3 78.4 %copy-start.13 = (f32[256]{0:T(256)}, f32[256]{0:T(256)S(1)}, u32[]{:S(2)}) copy-start(f32[256]{0:T(256)S(1)} %add_rsqrt_fusion.2) | copy-start | bytes 3076
  90.8 1.2 copy-start.6
  93.8 9.5 %copy-start.4 = (f32[256,384]{0,1:T(8,128)}, f32[256,384]{0,1:T(8,128)S(1)}, u32[]{:S(2)}) copy-start(f32[256,384]{0,1:T(8,128)S(1)} %copy.90) | copy-start | bytes 1179652
  103.3 121.7 %reduce-scatter.3.cloned.1.call-start = ((), (), s32[]{:S(2)}) async-start(), calls=%async_computation.6 | async-start | bytes 3538944 | tf_op jit(solution)/shard_map/reduce_scatter | solution.py:141
  157.0 2.8 copy-start.10
  159.8 2.6 copy-start.3
  166.8 1.6 copy-start.2
  179.3 225.0 %reduce-scatter.5.cloned.1.call-start = ((), (), s32[]{:S(2)}) async-start(), calls=%async_computation.7 | async-start | bytes 9732096 | tf_op jit(solution)/shard_map/reduce_scatter | solution.py:178
  183.9 44.9 %copy-start.5 = (f32[256,384]{0,1:T(8,128)S(1)}, f32[256,384]{0,1:T(8,128)}, u32[]{:S(2)}) copy-start(f32[256,384]{0,1:T(8,128)} %copy-done.4) | copy-start | bytes 1179652
  231.9 8.9 %copy-start.12 = (f32[256]{0:T(256)S(1)}, f32[256]{0:T(256)}, u32[]{:S(2)}) copy-start(f32[256]{0:T(256)} %copy-done.11) | copy-start | bytes 3076
  231.9 8.9 %copy-start.14 = (f32[256]{0:T(256)S(1)}, f32[256]{0:T(256)}, u32[]{:S(2)}) copy-start(f32[256]{0:T(256)} %copy-done.13) | copy-start | bytes 3076
  236.1 0.7 copy-start.7
  254.9 0.9 copy-start.8
  254.9 1.0 copy-start.9
  262.6 27.2 %all-to-all-start = ((bf16[8,256,384]{2,1,0:T(8,128)(2,1)}), bf16[8,256,384]{2,1,0:T(8,128)(2,1)}, u32[]{:S(2)}, u32[]{:S(2)}) async-start(bf16[8,256,384]{2,1,0:T(8,128)(2,1)} %bitcast.107), calls=%async_computation.2 | async-start | bytes 3145728 | tf_op jit(solution)/shard_map/all_to_all | solution.py:26
Sparse Core Ops, SparseCore 0:
  10.4 75.0 all-gather.2
  103.4 44.4 all-gather.4
  179.4 45.5 reduce-scatter.2
  255.1 149.1 reduce-scatter.4
where the time goes:
time: 415 us; the launch traced here: 414 us
  waiting for transfers between devices  264 us (64%)
  local copies, waits for them, and re-layouts  42.5 us (10%)
  matrix products  37.9 us (9%)
  other arithmetic  35.6 us (9%)
  between operations  14 us (3%)
  blocking collectives  12 us (3%)
  starting transfers between devices  7.64 us (2%)
    reduce_scatter x1, waiting for transfers between devices, local(): lax.psum_scatter(jnp.concatenate([qkv_term, out_term[:, None, :]], axis=1...  97.6 us
    all_gather x1, waiting for transfers between devices, sent_together(): result, at, done = (lax.all_gather(both, axis, axis=dim, tiled=True), 0, [])  73.2 us
    all_gather x1, waiting for transfers between devices, local(): every_pair = lax.all_gather(key_value, 'seq', axis=1, tiled=True)  40.1 us
    reduce_scatter x1, waiting for transfers between devices, local(): lax.psum_scatter(every_grad.astype(jnp.bfloat16), 'seq', scatter_dimensio...  36 us
    all_to_all x1, waiting for transfers between devices, summed_on_arrival(): pieces = lax.all_to_all(split_up(shard, dim, size), axis, 0, 0, tiled=True)  17.6 us
    all_to_all x1, blocking collectives, copy_for_each(): return lax.all_to_all(copies, axis, split_axis=0, concat_axis=0, tiled=True)  12 us
    concatenate x1, other arithmetic, local(): jnp.concatenate([qkv_term, out_term[:, None, :]], axis=1)  8.45 us
  transfers between devices with their start and end apart: 5, of which 5 were waited for; matrix products, arithmetic and copies ran while one was open for 7% of the time, Pallas kernels for 0%

commit v1 on v0

--- a/solution.py
+++ b/solution.py
@@ -104,7 +104,9 @@
             * score_scale
         )
 
-    every_pair = lax.all_gather(key_value, "seq", axis=1, tiled=True)
+    every_pair = jnp.concatenate(
+        lax.all_to_all(jnp.stack([key_value] * lax.axis_size("seq")), "seq", 0, 0), axis=1
+    )
     piece_rows = every_pair.shape[1]
     exponent = jnp.exp(scores_of(every_pair[0]))
     add_exp_total = jnp.sum(exponent, axis=-1)

time: 415 us -> 461 us (1.11)
  waiting for transfers between devices: 264 us -> 292 us
  local copies, waits for them, and re-layouts: 42.5 us -> 54.6 us
  starting transfers between devices: 7.64 us -> 12.7 us
    all_to_all x0 -> x1, waiting for transfers between devices: none -> 69.6 us  [local(): lax.all_to_all(jnp.stack([key_value] * lax.axis_size('seq')), 'seq', 0, 0)]
    all_gather x1 -> x0, waiting for transfers between devices: 40.1 us -> none  [local(): every_pair = lax.all_gather(key_value, 'seq', axis=1, tiled=True)]
    another operation x0 -> x3, local copies, waits for them, and re-layouts: none -> 10.5 us  [the longest x1 3.77 us: local(): value_rows = every_pair[1].reshape(piece_rows, head_count, HD)]
    all_to_all x0 -> x1, starting transfers between devices: none -> 5 us  [local(): lax.all_to_all(jnp.stack([key_value] * lax.axis_size('seq')), 'seq', 0, 0)]
where the time goes in v1:
time: 461 us; the launch traced here: 458 us
  waiting for transfers between devices  292 us (63%)
  local copies, waits for them, and re-layouts  54.6 us (12%)
  matrix products  37.9 us (8%)
  other arithmetic  35.6 us (8%)
  between operations  14 us (3%)
  starting transfers between devices  12.7 us (3%)
  blocking collectives  11.8 us (3%)
    reduce_scatter x1, waiting for transfers between devices, local(): lax.psum_scatter(jnp.concatenate([qkv_term, out_term[:, None, :]], axis=1...  97.4 us
    all_gather x1, waiting for transfers between devices, sent_together(): result, at, done = (lax.all_gather(both, axis, axis=dim, tiled=True), 0, [])  73.2 us
    all_to_all x1, waiting for transfers between devices, local(): lax.all_to_all(jnp.stack([key_value] * lax.axis_size('seq')), 'seq', 0, 0)  69.6 us
    reduce_scatter x1, waiting for transfers between devices, local(): lax.psum_scatter(every_grad.astype(jnp.bfloat16), 'seq', scatter_dimensio...  33.8 us
    all_to_all x1, waiting for transfers between devices, summed_on_arrival(): pieces = lax.all_to_all(split_up(shard, dim, size), axis, 0, 0, tiled=True)  17.7 us
    all_to_all x1, blocking collectives, copy_for_each(): return lax.all_to_all(copies, axis, split_axis=0, concat_axis=0, tiled=True)  11.8 us
  transfers between devices with their start and end apart: 5, of which 5 were waited for; matrix products, arithmetic and copies ran while one was open for 7% of the time, Pallas kernels for 0%

profile of v1, /device:TPU:16, one launch (start us, length us, event | category | flops | bytes accessed | tf_op | source)
XLA Modules:
  0.0 458.3 jit_solution(9835672840156518721)
XLA Ops:
  12.3 73.2 %all-gather.2.cloned.1.call-done = bf16[3072,1536]{1,0:T(8,128)(2,1)} async-done(((bf16[96,1536]{1,0:T(8,128)(2,1)}), bf16[3072,1536]{1,0:T(8,128)(2,1)}) %all-gather.2.cloned.1.call-update) | async-done | bytes 9437200 | tf_op jit(solution)/shard_map/all_gather | solution.py:12
  85.5 5.3 %fusion.2 = f32[256,1152]{1,0:T(8,128)S(1)} fusion(bf16[3072,1536]{1,0:T(8,128)(2,1)} %all-gather.2.cloned.1.call-done, bf16[1,256,3072]{2,1,0:T(8,128)(2,1)S(1)} %copy-done.1, f32[256]{0:T(256)S(1)} %add_rsqrt_fusion.2, f32[256]{0:T(256)S(1)} %broadcast_multiply_fusion.6), kind=kOutput, calls=%fused_computation.5 | convolution fusion | flops 1815085056 | bytes 9832448 | tf_op jit(solution)/shard_map/dot_general | solution.py:76
  105.2 3.0 stack.11
  108.1 5.0 %all-to-all-start = ((bf16[8,2,256,384]{2,3,1,0:T(8,128)(2,1)}), bf16[8,2,256,384]{2,3,1,0:T(8,128)(2,1)}, u32[]{:S(2)}, u32[]{:S(2)}) async-start(bf16[8,2,256,384]{2,3,1,0:T(8,128)(2,1)} %stack.11), calls=%async_computation | async-start | bytes 6291456 | tf_op jit(solution)/shard_map/all_to_all | solution.py:108
  114.7 3.2 fusion.38
  117.8 69.6 %all-to-all-done = bf16[8,2,256,384]{2,3,1,0:T(8,128)(2,1)} async-done(((bf16[8,2,256,384]{2,3,1,0:T(8,128)(2,1)}), bf16[8,2,256,384]{2,3,1,0:T(8,128)(2,1)}, u32[]{:S(2)}, u32[]{:S(2)}) %all-to-all-start) | async-done | bytes 3145760 | tf_op jit(solution)/shard_map/all_to_all | solution.py:108
  187.4 3.4 fusion.64
  192.8 3.7 reshape_squeeze.14
  196.6 3.4 copy.97
  200.0 3.8 reshape_squeeze.15
  203.8 2.8 fusion.6
  206.6 2.6 fusion.22
  216.9 2.6 copy.100
  222.1 3.9 pad_maximum_fusion.1
  226.3 3.6 fusion.63
  232.5 3.4 fusion.7
  235.8 33.8 %reduce-scatter.3.cloned.1.call-done = bf16[2,256,384]{2,1,0:T(8,128)(2,1)} async-done(((bf16[2,2048,384]{2,1,0:T(8,128)(2,1)}), bf16[2,256,384]{2,1,0:T(8,128)(2,1)}) %reduce-scatter.3.cloned.1.call-update) | async-done | bytes 393232 | tf_op jit(solution)/shard_map/reduce_scatter | solution.py:143
  285.4 5.7 %convolution_convert_fusion = bf16[3072,3,384]{2,0,1:T(8,128)(2,1)} fusion(bf16[3,384,256]{2,1,0:T(8,128)(2,1)} %bitcast.117, bf16[1,256,3072]{2,1,0:T(8,128)(2,1)S(1)} %copy-done.1, f32[256]{0:T(256)S(1)} %copy-done.14, f32[256]{0:T(256)S(1)} %copy-done.12), kind=kOutput, calls=%fused_computation.7 | convolution fusion | flops 1818624000 | bytes 9242624 | tf_op jit(solution)/shard_map/rd,rc->dc/dot_general | solution.py:174
  291.1 8.4 %pad_maximum_fusion = bf16[3072,4,384]{2,0,1:T(8,128)(2,1)} fusion(bf16[3072,1,384]{2,0,1:T(8,128)(2,1)} %fusion.7, bf16[3072,3,384]{2,0,1:T(8,128)(2,1)} %convolution_convert_fusion), kind=kLoop, calls=%fused_computation | loop fusion | flops 4718592 | bytes 18874368 | tf_op jit(solution)/shard_map/concatenate | solution.py:181
  300.5 5.3 %fusion.8 = bf16[256,3072]{1,0:T(8,128)(2,1)S(1)} fusion(bf16[3072,1536]{1,0:T(8,128)(2,1)} %all-gather.2.cloned.1.call-done, bf16[256,384]{1,0:T(8,128)(2,1)} %get-tuple-element.14, bf16[256,384]{1,0:T(8,128)(2,1)S(1)} %copy-done.8, bf16[256,384]{1,0:T(8,128)(2,1)S(1)} %copy-done.9), kind=kOutput, calls=%fused_computation.18 | convolution fusion | flops 1814495232 | bytes 9240576 | tf_op jit(solution)/shard_map/rc,dc->rd/dot_general | solution.py:156
  307.2 7.2 %all-to-all-start.1 = ((bf16[8,256,384]{2,1,0:T(8,128)(2,1)}), bf16[8,256,384]{2,1,0:T(8,128)(2,1)}, u32[]{:S(2)}, u32[]{:S(2)}) async-start(bf16[8,256,384]{2,1,0:T(8,128)(2,1)} %bitcast.112), calls=%async_computation.3 | async-start | bytes 3145728 | tf_op jit(solution)/shard_map/all_to_all | solution.py:26
  316.7 17.7 %all-to-all-done.1 = bf16[8,256,384]{2,1,0:T(8,128)(2,1)} async-done(((bf16[8,256,384]{2,1,0:T(8,128)(2,1)}), bf16[8,256,384]{2,1,0:T(8,128)(2,1)}, u32[]{:S(2)}, u32[]{:S(2)}) %all-to-all-start.1) | async-done | bytes 1572896 | tf_op jit(solution)/shard_map/all_to_all | solution.py:26
  337.4 11.8 %all_to_all.16 = f32[8,1,512]{2,1,0:T(1,128)S(1)} all-to-all(f32[8,1,512]{2,1,0:T(1,128)S(1)} %broadcast_in_dim.8), channel_id=1, replica_groups=mesh['seq'=8,'tensor'=8,'dp'=4] {'tensor'}, dimensions={0} | all-to-all | bytes 32768 | tf_op jit(solution)/shard_map/all_to_all | solution.py:32
  351.0 97.4 %reduce-scatter.5.cloned.1.call-done = bf16[96,4,384]{2,0,1:T(8,128)(2,1)} async-done(((bf16[3072,4,384]{2,0,1:T(8,128)(2,1)}), bf16[96,4,384]{2,0,1:T(8,128)(2,1)}) %reduce-scatter.5.cloned.1.call-update) | async-done | bytes 294928 | tf_op jit(solution)/shard_map/reduce_scatter | solution.py:180
  (92 shorter events, 64.6 us)
Async XLA Ops:
  7.2 107.5 %copy-start = (bf16[1,256,3072]{2,1,0:T(8,128)(2,1)S(1)}, bf16[1,256,3072]{2,1,0:T(8,128)(2,1)}, u32[]{:S(2)}) copy-start(bf16[1,256,3072]{2,1,0:T(8,128)(2,1)} %param.5) | copy-start | bytes 4718596
  7.2 4.5 copy-start.1
  7.2 78.3 %all-gather.2.cloned.1.call-start = ((), (), s32[]{:S(2)}) async-start(), calls=%async_computation.5 | async-start | bytes 9732096 | tf_op jit(solution)/shard_map/all_gather | solution.py:12
  11.7 79.1 %copy-start.11 = (f32[256]{0:T(256)}, f32[256]{0:T(256)S(1)}, u32[]{:S(2)}) copy-start(f32[256]{0:T(256)S(1)} %broadcast_multiply_fusion.6) | copy-start | bytes 3076
  12.3 78.5 %copy-start.13 = (f32[256]{0:T(256)}, f32[256]{0:T(256)S(1)}, u32[]{:S(2)}) copy-start(f32[256]{0:T(256)S(1)} %add_rsqrt_fusion.2) | copy-start | bytes 3076
  90.8 1.2 copy-start.6
  93.8 11.3 %copy-start.4 = (f32[256,384]{0,1:T(8,128)}, f32[256,384]{0,1:T(8,128)S(1)}, u32[]{:S(2)}) copy-start(f32[256,384]{0,1:T(8,128)S(1)} %copy.89) | copy-start | bytes 1179652
  108.1 79.3 %all-to-all-start = ((bf16[8,2,256,384]{2,3,1,0:T(8,128)(2,1)}), bf16[8,2,256,384]{2,3,1,0:T(8,128)(2,1)}, u32[]{:S(2)}, u32[]{:S(2)}) async-start(bf16[8,2,256,384]{2,3,1,0:T(8,128)(2,1)} %stack.11), calls=%async_computation | async-start | bytes 6291456 | tf_op jit(solution)/shard_map/all_to_all | solution.py:108
  113.1 156.5 %reduce-scatter.3.cloned.1.call-start = ((), (), s32[]{:S(2)}) async-start(), calls=%async_computation.6 | async-start | bytes 3538944 | tf_op jit(solution)/shard_map/reduce_scatter | solution.py:143
  203.8 2.8 copy-start.10
  206.6 2.6 copy-start.3
  213.5 1.6 copy-start.2
  226.1 222.4 %reduce-scatter.5.cloned.1.call-start = ((), (), s32[]{:S(2)}) async-start(), calls=%async_computation.7 | async-start | bytes 9732096 | tf_op jit(solution)/shard_map/reduce_scatter | solution.py:180
  230.7 42.7 %copy-start.5 = (f32[256,384]{0,1:T(8,128)S(1)}, f32[256,384]{0,1:T(8,128)}, u32[]{:S(2)}) copy-start(f32[256,384]{0,1:T(8,128)} %copy-done.4) | copy-start | bytes 1179652
  276.5 8.9 %copy-start.12 = (f32[256]{0:T(256)S(1)}, f32[256]{0:T(256)}, u32[]{:S(2)}) copy-start(f32[256]{0:T(256)} %copy-done.11) | copy-start | bytes 3076
  276.5 8.9 %copy-start.14 = (f32[256]{0:T(256)S(1)}, f32[256]{0:T(256)}, u32[]{:S(2)}) copy-start(f32[256]{0:T(256)} %copy-done.13) | copy-start | bytes 3076
  280.7 0.7 copy-start.7
  299.5 0.9 copy-start.8
  299.5 1.0 copy-start.9
  307.2 27.2 %all-to-all-start.1 = ((bf16[8,256,384]{2,1,0:T(8,128)(2,1)}), bf16[8,256,384]{2,1,0:T(8,128)(2,1)}, u32[]{:S(2)}, u32[]{:S(2)}) async-start(bf16[8,256,384]{2,1,0:T(8,128)(2,1)} %bitcast.112), calls=%async_computation.3 | async-start | bytes 3145728 | tf_op jit(solution)/shard_map/all_to_all | solution.py:26
Sparse Core Ops, SparseCore 0:
  10.4 75.0 all-gather.1
  226.2 43.4 reduce-scatter.2
  299.7 148.6 reduce-scatter.4
